TPU v7x, 32 devices: a whole 2x2x4 slice. The times are simulated.
32 devices in a mesh: pair: 4 (over x, core), aux: 8 (over z, y).
Axes of the slice: x: 2, y: 2, z: 4, core: 2. Of those that a mesh axis runs over, the one named last changes fastest.
Arguments:
- left_active: bfloat16 [40, 128, 61440], P('pair', None, 'aux'), may hold values from -0.375 to 0.375
- right_active: bfloat16 [40, 128, 61440], P('pair', None, 'aux'), may hold values from -0.375 to 0.375
- amps_active: bfloat16 [40, 128, 128], P('pair', 'aux'), may hold values from -0.5 to 0.5
- rank_active: int32 [40], P('pair'), may hold values from 80 to 128, as said below
- gap_active: float32 [40], P('pair'), may hold values from 0.5 to 2
- energy_active: float32 [40, 128], P('pair'), may hold values from 0.5 to 4
- intersect_active: bfloat16 [40, 4, 128, 128], P('pair'), may hold values from -0.75 to 0.75
- fock_active: float32 [40, 4], P('pair'), may hold values from -2 to 2
- neighbor_active: int32 [40, 4], P('pair'), may hold values from 0 to 39
- left_env: bfloat16 [16, 48, 61440], P('pair', None, 'aux'), may hold values from -0.375 to 0.375
- right_env: bfloat16 [16, 48, 61440], P('pair', None, 'aux'), may hold values from -0.375 to 0.375
- amps_env: bfloat16 [16, 48, 48], P('pair', 'aux'), may hold values from -0.875 to 0.875
- rank_env: int32 [16], P('pair'), may hold values from 24 to 48, as said below
- gap_env: float32 [16], P('pair'), may hold values from 0.5 to 2
- energy_env: float32 [16, 48], P('pair'), may hold values from 0.5 to 4
- intersect_env: bfloat16 [16, 4, 48, 48], P('pair'), may hold values from -1.25 to 1.25
- fock_env: float32 [16, 4], P('pair'), may hold values from -2 to 2
- neighbor_env: int32 [16, 4], P('pair'), may hold values from 0 to 15
Outputs:
- new_active: float32 [40, 128, 128], P('pair', 'aux')
- new_env: float32 [16, 48, 48], P('pair', 'aux')
Inputs may be any that keep to these rules, and one draw needn't show every extreme that they name: `rank_active`: multiples of 8; the first active pair has rank 128. `rank_env`: multiples of 8; the first environment pair has rank 48.
All inputs are finite; a program needn't handle non-finite values.
Results may differ from a plain program's by a relative error of at most 0.0041.
Values may be sent and summed in bfloat16 or wider, within the bound.
A program may use at most 128 MiB of HBM per device.

v0:
```python
import jax
import jax.numpy as jnp
from jax import lax
from jax.sharding import PartitionSpec as P

HIGHEST = lax.Precision.HIGHEST


def shard_mask(pair_ranks, row_count, full_width, row_start):
    row_index = row_start + jnp.arange(row_count, dtype=jnp.int32)
    col_index = jnp.arange(full_width, dtype=jnp.int32)
    return (row_index[None, :, None] < pair_ranks[:, None, None]) & (
        col_index[None, None, :] < pair_ranks[:, None, None]
    )


def aux_terms(left_ints, right_ints, own_full, with_ladder):
    summed_terms = jnp.einsum(
        "paq,pbq->pab", left_ints, right_ints, preferred_element_type=jnp.float32
    )
    if with_ladder:
        cross_left = jnp.einsum(
            "pab,paq->pbq", own_full, left_ints, preferred_element_type=jnp.float32
        ).astype(jnp.bfloat16)
        cross_right = jnp.einsum(
            "pab,pbq->paq", own_full, right_ints, preferred_element_type=jnp.float32
        ).astype(jnp.bfloat16)
        summed_terms = summed_terms + jnp.einsum(
            "pcq,pbq->pcb", cross_left, right_ints, preferred_element_type=jnp.float32
        )
        summed_terms = summed_terms + jnp.einsum(
            "pcq,paq->pca", cross_left, cross_right, preferred_element_type=jnp.float32
        )
    return summed_terms


def couple_blocks(cols_over, near_block, intersect, fock_weights):
    right_part = jnp.einsum(
        "pkst,pkut->pksu", near_block, intersect, preferred_element_type=jnp.float32
    )
    right_part = right_part * fock_weights[:, :, None, None]
    return jnp.einsum(
        "pkrs,pksu->pru", cols_over.astype(jnp.float32), right_part, precision=HIGHEST
    )


def finish(summed, amp_shard, pair_ranks, pair_gaps, energy, row_start):
    row_count = amp_shard.shape[1]
    inside = shard_mask(pair_ranks, row_count, amp_shard.shape[2], row_start)
    energy_rows = lax.dynamic_slice_in_dim(energy, row_start, row_count, 1)
    denominator = energy_rows[:, :, None] + energy[:, None, :] + pair_gaps[:, None, None]
    return jnp.where(inside, amp_shard.astype(jnp.float32) - summed / denominator, jnp.float32(0.0))


def shards(
    left_active,
    right_active,
    amps_active,
    rank_active,
    gap_active,
    energy_active,
    intersect_active,
    fock_active,
    neighbor_active,
    left_env,
    right_env,
    amps_env,
    rank_env,
    gap_env,
    energy_env,
    intersect_env,
    fock_env,
    neighbor_env,
):
    aux_place = lax.axis_index("aux")
    rows_act = amps_active.shape[1]
    rows_env = amps_env.shape[1]
    start_act = aux_place * rows_act
    start_env = aux_place * rows_env
    shard_act = jnp.where(
        shard_mask(rank_active, rows_act, amps_active.shape[2], start_act),
        amps_active,
        jnp.zeros_like(amps_active),
    )
    shard_env = jnp.where(
        shard_mask(rank_env, rows_env, amps_env.shape[2], start_env),
        amps_env,
        jnp.zeros_like(amps_env),
    )
    own_act = lax.all_gather(shard_act, "aux", axis=1, tiled=True)
    block_act, block_env = (
        lax.all_gather(shard_act, "pair", axis=0, tiled=True),
        lax.all_gather(shard_env, "pair", axis=0, tiled=True),
    )
    cols_over_act = lax.dynamic_slice_in_dim(intersect_active, start_act, rows_act, 3)
    cols_over_env = lax.dynamic_slice_in_dim(intersect_env, start_env, rows_env, 3)
    terms_act = aux_terms(left_active, right_active, own_act, True) + couple_blocks(
        cols_over_act, block_act[neighbor_active], intersect_active, fock_active
    )
    terms_env = aux_terms(left_env, right_env, None, False) + couple_blocks(
        cols_over_env, block_env[neighbor_env], intersect_env, fock_env
    )
    summed_act, summed_env = (
        lax.psum_scatter(terms_act, "aux", scatter_dimension=1, tiled=True),
        lax.psum_scatter(terms_env, "aux", scatter_dimension=1, tiled=True),
    )
    new_active = finish(summed_act, shard_act, rank_active, gap_active, energy_active, start_act)
    new_env = finish(summed_env, shard_env, rank_env, gap_env, energy_env, start_env)
    return (new_active, new_env)


def solution(mesh):
    return jax.shard_map(
        shards,
        mesh=mesh,
        in_specs=(
            P("pair", None, "aux"),
            P("pair", None, "aux"),
            P("pair", "aux", None),
            P("pair"),
            P("pair"),
            P("pair", None),
            P("pair", None, None, None),
            P("pair", None),
            P("pair", None),
            P("pair", None, "aux"),
            P("pair", None, "aux"),
            P("pair", "aux", None),
            P("pair"),
            P("pair"),
            P("pair", None),
            P("pair", None, None, None),
            P("pair", None),
            P("pair", None),
        ),
        out_specs=(P("pair", "aux", None), P("pair", "aux", None)),
        check_vma=False,
    )
```

profile of v0, /device:TPU:0, one launch (start us, length us, event | category | flops | bytes accessed | tf_op | source)
XLA Modules:
  0.0 192.5 jit_solution(5022466453750322874)
XLA Ops:
  7.2 0.0 copy-start
  7.2 0.0 reduce-scatter.2.cloned.1.call-start
  7.2 0.9 iota_compare_fusion
  8.1 0.7 broadcast_compare_fusion
  8.9 0.9 and_select_fusion.1
  9.7 32.7 %all_gather.9 = bf16[10,128,128]{2,1,0:T(8,128)(2,1)S(1)} all-gather(bf16[10,16,128]{2,1,0:T(8,128)(2,1)S(1)} %and_select_fusion.1), channel_id=1, replica_groups=mesh['pair'=4,'aux'=8] {'aux'}, dimensions={1}, use_global_device_ids=true | all-gather | bytes 368640 | tf_op jit(solution)/shard_map/all_gather | solution.py:90
  42.4 5.9 %all_gather.10 = bf16[40,16,128]{2,1,0:T(8,128)(2,1)} all-gather(bf16[10,16,128]{2,1,0:T(8,128)(2,1)S(1)} %and_select_fusion.1), channel_id=1, replica_groups=mesh['pair'=4,'aux'=8] {'pair'}, dimensions={0}, use_global_device_ids=true | all-gather | bytes 204800 | tf_op jit(solution)/shard_map/all_gather | solution.py:92
  48.3 13.3 %convolution_convert_fusion = bf16[10,128,7680]{2,1,0:T(8,128)(2,1)} fusion(bf16[10,128,128]{2,1,0:T(8,128)(2,1)S(1)} %all_gather.9, bf16[10,128,7680]{2,1,0:T(8,128)(2,1)} %param.18), kind=kOutput, calls=%fused_computation.4 | convolution fusion | flops 2526412800 | bytes 39649280 | tf_op jit(solution)/shard_map/pab,paq->pbq/dot_general | solution.py:22
  61.6 15.7 %fusion.19 = f32[10,128,128]{2,1,0:T(8,128)} fusion(bf16[10,128,7680]{2,1,0:T(8,128)(2,1)} %param.18, bf16[10,128,7680]{2,1,0:T(8,128)(2,1)} %param.19), kind=kOutput, calls=%fused_computation.38 | convolution fusion | flops 2516582400 | bytes 39976960 | tf_op jit(solution)/shard_map/paq,pbq->pab/dot_general | solution.py:18
  77.3 16.0 %convolution_add_fusion = f32[10,128,128]{2,1,0:T(8,128)} fusion(f32[10,128,128]{2,1,0:T(8,128)} %fusion.19, bf16[10,128,7680]{2,1,0:T(8,128)(2,1)} %convolution_convert_fusion, bf16[10,128,7680]{2,1,0:T(8,128)(2,1)} %param.19), kind=kOutput, calls=%fused_computation.11 | convolution fusion | flops 2516746240 | bytes 40632320 | tf_op jit(solution)/shard_map/pcq,pbq->pcb/dot_general | solution.py:28
  93.3 0.0 copy-start.1
  93.3 0.0 copy-start.6
  93.3 0.0 copy-start.5
  93.3 0.0 copy-start.3
  93.3 0.0 copy-start.2
  93.4 17.9 %fusion.9 = f32[10,128,128]{2,1,0:T(8,128)} fusion(f32[10,128,128]{2,1,0:T(8,128)} %convolution_add_fusion, bf16[10,128,7680]{2,1,0:T(8,128)(2,1)} %convolution_convert_fusion, bf16[10,128,128]{2,1,0:T(8,128)(2,1)S(1)} %all_gather.9, bf16[10,128,7680]{2,1,0:T(8,128)(2,1)} %param.19), kind=kOutput, calls=%fused_computation.9 | convolution fusion | flops 5043159040 | bytes 40960000 | tf_op jit(solution)/shard_map/pcq,paq->pca/dot_general | solution.py:31
  111.2 0.0 copy-done.8
  111.2 0.1 copy.33
  111.3 0.1 reshape.128
  111.4 0.0 copy-done.7
  111.4 0.1 copy.34
  111.5 1.5 gather_fusion
  113.1 2.1 %convolution_multiply_fusion = f32[10,4,16,128]{3,2,1,0:T(8,128)S(1)} fusion(bf16[10,4,16,128]{3,2,1,0:T(8,128)(2,1)S(1)} %bitcast.28, bf16[10,4,128,128]{3,2,1,0:T(8,128)(2,1)} %param.24, f32[10,4]{1,0:T(8,128)S(1)} %copy.34), kind=kOutput, calls=%fused_computation.12 | convolution fusion | flops 21053440 | bytes 1802400 | tf_op jit(solution)/shard_map/pkst,pkut->pksu/dot_general | solution.py:38
  115.1 3.5 %fusion.12 = f32[10,128,128]{2,1,0:T(8,128)} fusion(f32[10,128,128]{2,1,0:T(8,128)} %fusion.9, f32[10,4,16,128]{3,2,1,0:T(8,128)S(1)} %convolution_multiply_fusion, bf16[10,4,128,128]{3,2,1,0:T(8,128)(2,1)} %param.24, s32[]{:T(128)S(6)} %select_n.31), kind=kOutput, calls=%fused_computation.10 | convolution fusion | flops 125992960 | bytes 2949124 | tf_op jit(solution)/shard_map/pkrs,pksu->pru/dot_general | solution.py:42
  118.6 0.0 reduce-scatter.2.cloned.1.call-update
  118.6 0.7 iota_compare_fusion.1
  119.4 0.7 broadcast_compare_fusion.1
  120.1 0.0 copy-done.4
  120.1 0.1 and_select_fusion.3
  120.2 5.2 %all_gather.11 = bf16[16,6,48]{2,1,0:T(8,128)(2,1)S(1)} all-gather(bf16[4,6,48]{2,1,0:T(8,128)(2,1)S(1)} %and_select_fusion.3), channel_id=1, replica_groups=mesh['pair'=4,'aux'=8] {'pair'}, dimensions={0}, use_global_device_ids=true | all-gather | bytes 11520 | tf_op jit(solution)/shard_map/all_gather | solution.py:93
  125.3 0.7 compare_select_fusion
  126.0 0.1 reshape.136
  126.1 0.6 gather_fusion.1
  126.7 0.0 copy-done.1
  126.7 0.2 convolution_multiply_fusion.1
  126.9 0.4 convolution_bitcast_fusion
  127.3 0.0 copy-done
  127.3 2.7 %convolution_add_fusion.1 = f32[4,48,48]{2,1,0:T(8,128)S(1)} fusion(f32[4,48,48]{2,1,0:T(8,128)S(1)} %convolution_bitcast_fusion, bf16[4,48,7680]{2,1,0:T(8,128)(2,1)S(1)} %copy-done, bf16[4,48,7680]{2,1,0:T(8,128)(2,1)} %param.28), kind=kOutput, calls=%fused_computation.14 | convolution fusion | flops 141566976 | bytes 5971968 | tf_op jit(solution)/shard_map/paq,pbq->pab/dot_general | solution.py:18
  130.1 1.2 dynamic-slice
  132.0 38.5 %all-reduce = f32[4,48,48]{2,0,1:T(4,128)S(1)} all-reduce(f32[4,48,48]{2,0,1:T(4,128)S(1)} %copy.37), channel_id=3, replica_groups=mesh['pair'=4,'aux'=8] {'aux'}, use_global_device_ids=true, to_apply=%region_1.2.clone | all-reduce | flops 9216 | bytes 73728
  170.5 0.0 copy-done.5
  170.5 0.1 constant_dynamic-slice_fusion
  170.6 0.7 and_select_fusion.2
  171.3 0.6 copy.39
  172.0 0.0 copy-done.3
  172.0 0.1 constant_dynamic-slice_fusion.1
  172.0 12.0 %reduce-scatter.2.cloned.1.call-done = f32[10,16,128]{2,1,0:T(8,128)} async-done(((f32[10,128,128]{2,1,0:T(8,128)}), f32[10,16,128]{2,1,0:T(8,128)}) %reduce-scatter.2.cloned.1.call-update) | async-done | bytes 81936 | tf_op jit(solution)/shard_map/reduce_scatter | solution.py:104
  184.0 1.6 and_select_fusion
  (12 shorter events, 0.1 us)
Async XLA Ops:
  7.2 120.2 %copy-start = (bf16[4,48,7680]{2,1,0:T(8,128)(2,1)S(1)}, bf16[4,48,7680]{2,1,0:T(8,128)(2,1)}, u32[]{:S(2)}) copy-start(bf16[4,48,7680]{2,1,0:T(8,128)(2,1)} %param.27) | copy-start | bytes 8847364
  7.2 176.9 %reduce-scatter.2.cloned.1.call-start = ((), (), s32[]{:S(2)}) async-start(), calls=%async_computation.1 | async-start | bytes 737280 | tf_op jit(solution)/shard_map/reduce_scatter | solution.py:104
  93.3 17.9 %copy-start.8 = (s32[10,4]{0,1:T(4,128)S(1)}, s32[10,4]{0,1:T(4,128)}, u32[]{:S(2)}) copy-start(s32[10,4]{0,1:T(4,128)} %param.26) | copy-start | bytes 484
  93.3 18.1 %copy-start.7 = (f32[10,4]{0,1:T(4,128)S(1)}, f32[10,4]{0,1:T(4,128)}, u32[]{:S(2)}) copy-start(f32[10,4]{0,1:T(4,128)} %param.25) | copy-start | bytes 484
  93.3 26.8 %copy-start.4 = (bf16[4,6,48]{2,0,1:T(4,128)(2,1)S(1)}, bf16[4,6,48]{2,0,1:T(4,128)(2,1)}, u32[]{:S(2)}) copy-start(bf16[4,6,48]{2,0,1:T(4,128)(2,1)} %param.29) | copy-start | bytes 6916
  93.3 33.4 %copy-start.1 = (bf16[4,4,48,48]{3,2,1,0:T(8,128)(2,1)S(1)}, bf16[4,4,48,48]{3,2,1,0:T(8,128)(2,1)}, u32[]{:S(2)}) copy-start(bf16[4,4,48,48]{3,2,1,0:T(8,128)(2,1)} %param.33) | copy-start | bytes 221188
  93.3 33.4 %copy-start.6 = (f32[4,4]{1,0:T(4,128)S(1)}, f32[4,4]{1,0:T(4,128)}, u32[]{:S(2)}) copy-start(f32[4,4]{1,0:T(4,128)} %param.34) | copy-start | bytes 196
  93.3 77.2 %copy-start.5 = (f32[4,48]{1,0:T(4,128)S(1)}, f32[4,48]{1,0:T(4,128)}, u32[]{:S(2)}) copy-start(f32[4,48]{1,0:T(4,128)} %param.32) | copy-start | bytes 2308
  93.3 78.6 %copy-start.3 = (f32[10,128]{1,0:T(8,128)S(1)}, f32[10,128]{1,0:T(8,128)}, u32[]{:S(2)}) copy-start(f32[10,128]{1,0:T(8,128)} %param.23) | copy-start | bytes 15364
  93.3 90.7 %copy-start.2 = (bf16[10,16,128]{2,1,0:T(8,128)(2,1)S(1)}, bf16[10,16,128]{2,1,0:T(8,128)(2,1)}, u32[]{:S(2)}) copy-start(bf16[10,16,128]{2,1,0:T(8,128)(2,1)} %param.20) | copy-start | bytes 122884
Sparse Core Ops, SparseCore 0:
  118.7 65.2 reduce-scatter.1
where the time goes:
time: 193 us
  blocking collectives  82.3 us (43%)
  matrix products  71.7 us (37%)
  between operations  14.9 us (8%)
  waiting for transfers between devices  12 us (6%)
  other arithmetic  7.1 us (4%)
  local copies, waits for them, and re-layouts  4.54 us (2%)
    unnamed x1, blocking collectives  38.5 us
    all_gather x1, blocking collectives, shards(): own_act = lax.all_gather(shard_act, 'aux', axis=1, tiled=True)  32.7 us
    dot_general x2, matrix products, aux_terms(): jnp.einsum('paq,pbq->pab', left_ints, right_ints, preferred_element_type=...  18.5 us
    dot_general x1, matrix products, aux_terms(): jnp.einsum('pcq,paq->pca', cross_left, cross_right, preferred_element_typ...  17.9 us
    dot_general x1, matrix products, aux_terms(): jnp.einsum('pcq,pbq->pcb', cross_left, right_ints, preferred_element_type...  16 us
    dot_general x1, matrix products, aux_terms(): jnp.einsum('pab,paq->pbq', own_full, left_ints, preferred_element_type=jn...  13.3 us
    reduce_scatter x1, waiting for transfers between devices, shards(): lax.psum_scatter(terms_act, 'aux', scatter_dimension=1, tiled=True)  12 us
    all_gather x1, blocking collectives, shards(): lax.all_gather(shard_act, 'pair', axis=0, tiled=True)  5.94 us
  transfers between devices with their start and end apart: 1, of which 1 were waited for; matrix products, arithmetic and copies ran while one was open for 5% of the time, Pallas kernels for 0%

commit v1 on v0

v1 whole, which is shorter than its diff:
```python
import functools

import jax
import jax.numpy as jnp
from jax import lax
from jax.experimental import pallas as pl
from jax.experimental.pallas import tpu as pltpu
from jax.sharding import PartitionSpec as P

BF = jnp.bfloat16
F32 = jnp.float32
LANES = 128
AHEAD = 4


def dot_nt(x, y):
    return lax.dot_general(x, y, (((1,), (1,)), ((), ())), preferred_element_type=F32)


def split(x):
    hi = x.astype(BF)
    return hi, (x - hi.astype(F32)).astype(BF)


def iota2(shape, dim):
    return lax.broadcasted_iota(jnp.int32, shape, dim)


def couple(over, near, fock, place, rows, step):
    count = len(over)
    width = over[0].shape[1]
    pick = (iota2((step, width), 1) == place * rows + iota2((step, width), 0)) & (
        iota2((step, width), 0) < rows
    )
    pick = jnp.where(pick, F32(1.0), F32(0.0))
    both = None
    for k in range(count):
        above = [jnp.zeros((step * k, width), F32)] if k else []
        below = [jnp.zeros((LANES - step * (k + 1), width), F32)]
        weights = jnp.concatenate(above + [near[k]] + below + above + [pick] + below, axis=0)
        part = dot_nt(over[k], weights.astype(BF))
        both = part if both is None else both + part
    lane = iota2((1, LANES), 1)
    scale = jnp.zeros((1, LANES), F32)
    for k in range(count):
        scale = jnp.where((lane >= step * k) & (lane < step * (k + 1)), fock[k], scale)
    hi, lo = split(both[:, :LANES] * scale)
    cols = both[:, LANES:].astype(BF)
    return dot_nt(jnp.concatenate([cols, cols], axis=1), jnp.concatenate([hi, lo], axis=1))


def kernel(
    n_pair, n_aux,
    la, ra, aa, rka, gpa, ena, ina, fka, nba,
    le, re, ae, rke, gpe, ene, ine, fke, nbe,
    oa, oe,
    lbuf, rbuf, lebuf, rebuf, inbuf,
    mine, own, around, mine_e, around_e,
    terms, out_a, in_a, terms_e, out_e, in_e, den, den_e,
    lr_sem, lre_sem, in_sem,
    own_send, own_recv, pair_send, pair_recv, paire_send, paire_recv,
    a_send, a_recv, e_send, e_recv,
):
    pairs, rows, full = aa.shape
    pairs_e, rows_e, full_e = ae.shape
    pad_e = mine_e.shape[1]
    count = nba.shape[1]
    me = lax.axis_index("aux")
    my_pair = lax.axis_index("pair")

    def load_lr(p):
        return (
            pltpu.make_async_copy(la.at[p], lbuf.at[p], lr_sem.at[p, 0]),
            pltpu.make_async_copy(ra.at[p], rbuf.at[p], lr_sem.at[p, 1]),
        )

    load_e = (
        pltpu.make_async_copy(le, lebuf, lre_sem.at[0]),
        pltpu.make_async_copy(re, rebuf, lre_sem.at[1]),
    )
    load_in = pltpu.make_async_copy(ina, inbuf, in_sem)
    for copy in load_e:
        copy.start()
    load_in.start()
    for p in range(min(AHEAD, pairs)):
        for copy in load_lr(p):
            copy.start()

    barrier = pltpu.get_barrier_semaphore()
    for d in range(1, n_aux):
        pl.semaphore_signal(barrier, inc=1, device_id={"aux": lax.rem(me + d, n_aux)}, device_id_type=pl.DeviceIdType.MESH)
    for d in range(1, n_pair):
        pl.semaphore_signal(barrier, inc=1, device_id={"pair": lax.rem(my_pair + d, n_pair)}, device_id_type=pl.DeviceIdType.MESH)

    def inside(rank, start, shape):
        return (start + iota2(shape, 0) < rank) & (iota2(shape, 1) < rank)

    for p in range(pairs):
        keep = inside(rka[p], me * rows, (rows, full))
        block = jnp.where(keep, aa[p].astype(F32), F32(0.0)).astype(BF)
        mine[p] = block
        own[me, p] = block
        around[my_pair * pairs + p] = block
    mine_e[...] = jnp.zeros(mine_e.shape, F32)
    for p in range(pairs_e):
        keep = inside(rke[p], me * rows_e, (rows_e, full_e))
        mine_e[p, :rows_e, :full_e] = jnp.where(keep, ae[p].astype(F32), F32(0.0))
    for p in range(pairs_e):
        around_e[my_pair * pairs_e + p] = mine_e[p]
    out_e[...] = jnp.zeros(out_e.shape, F32)

    def to_own(d, slot):
        return pltpu.make_async_remote_copy(
            src_ref=mine, dst_ref=own.at[slot],
            send_sem=own_send.at[d - 1], recv_sem=own_recv.at[d - 1],
            device_id={"aux": lax.rem(me + d, n_aux)}, device_id_type=pl.DeviceIdType.MESH,
        )

    def to_pair(d, slot):
        return pltpu.make_async_remote_copy(
            src_ref=mine, dst_ref=around.at[pl.ds(slot * pairs, pairs)],
            send_sem=pair_send.at[d - 1], recv_sem=pair_recv.at[d - 1],
            device_id={"pair": lax.rem(my_pair + d, n_pair)}, device_id_type=pl.DeviceIdType.MESH,
        )

    def to_pair_e(d, slot):
        return pltpu.make_async_remote_copy(
            src_ref=mine_e, dst_ref=around_e.at[pl.ds(slot * pairs_e, pairs_e)],
            send_sem=paire_send.at[d - 1], recv_sem=paire_recv.at[d - 1],
            device_id={"pair": lax.rem(my_pair + d, n_pair)}, device_id_type=pl.DeviceIdType.MESH,
        )

    pl.semaphore_wait(barrier, n_aux - 1 + n_pair - 1)
    for d in range(1, n_pair):
        to_pair(d, my_pair).start()
        to_pair_e(d, my_pair).start()
    for d in range(1, n_aux):
        to_own(d, me).start()

    def denominators(energy, gap, start, height, wide):
        line = energy + jnp.zeros((height, wide), F32)
        diag = iota2((height, wide), 1) == start + iota2((height, wide), 0)
        mine_rows = jnp.sum(jnp.where(diag, line, F32(0.0)), axis=1, keepdims=True)
        return line + mine_rows + gap

    for p in range(pairs):
        den[p] = denominators(ena[pl.ds(p, 1), :], gpa[p], me * rows, rows, full)
    for p in range(pairs_e):
        den_e[p] = denominators(ene[pl.ds(p, 1), :], gpe[p], me * rows_e, rows_e, full_e)

    for copy in load_e:
        copy.wait()
    for p in range(pairs_e):
        terms_e[p] = dot_nt(lebuf[p], rebuf[p])

    def a_copy(d, p):
        peer = lax.rem(me + d, n_aux)
        return pltpu.make_async_remote_copy(
            src_ref=out_a.at[peer, p], dst_ref=in_a.at[d - 1, p],
            send_sem=a_send.at[d - 1], recv_sem=a_recv.at[d - 1],
            device_id={"aux": peer}, device_id_type=pl.DeviceIdType.MESH,
        )

    def e_copy(d):
        peer = lax.rem(me + d, n_aux)
        return pltpu.make_async_remote_copy(
            src_ref=out_e.at[peer], dst_ref=in_e.at[d - 1],
            send_sem=e_send.at[d - 1], recv_sem=e_recv.at[d - 1],
            device_id={"aux": peer}, device_id_type=pl.DeviceIdType.MESH,
        )

    def send_pair(p):
        for d in range(1, n_aux):
            a_copy(d, p).start()

    def step(p, carry):
        @pl.when(p + AHEAD < pairs)
        def _():
            for copy in load_lr(p + AHEAD):
                copy.start()

        for copy in load_lr(p):
            copy.wait()
        base = dot_nt(lbuf[p], rbuf[p])

        @pl.when(p == 0)
        def _():
            for d in range(1, n_pair):
                slot = lax.rem(my_pair + n_pair - d, n_pair)
                to_pair(d, slot).wait_recv()
                to_pair_e(d, slot).wait_recv()
            for d in range(1, n_aux):
                to_own(d, lax.rem(me + n_aux - d, n_aux)).wait_recv()
            load_in.wait()

        amps = own[:, p].astype(F32).reshape(full, full)
        flat = amps.astype(BF)
        turned = amps.T.astype(BF)
        hi, lo = split(base)
        half = base + (dot_nt(hi, flat) + dot_nt(lo, flat))
        hi, lo = split(half)
        total = base + jnp.dot(
            jnp.concatenate([turned, turned], axis=1),
            jnp.concatenate([hi, lo], axis=0),
            preferred_element_type=F32,
        )
        total = total + couple(
            [inbuf[p, k] for k in range(count)],
            [around[nba[p, k]].astype(F32) for k in range(count)],
            [fka[p, k] for k in range(count)],
            me, rows, rows,
        )
        terms[p] = total.reshape(n_aux, rows, full)
        for j in range(n_aux):
            out_a[j, p] = total[j * rows : (j + 1) * rows].astype(BF)

        @pl.when(p > 0)
        def _():
            send_pair(p - 1)

        @pl.when(p == 1)
        def _():
            for q in range(pairs_e):
                terms_e[q] = terms_e[q] + couple(
                    [ine[q, k] for k in range(count)],
                    [around_e[nbe[q, k]][:, :full_e] for k in range(count)],
                    [fke[q, k] for k in range(count)],
                    me, rows_e, pad_e,
                )
                for j in range(n_aux):
                    out_e[j, q, :rows_e, :full_e] = terms_e[q, j * rows_e : (j + 1) * rows_e, :]

        @pl.when(p == 2)
        def _():
            for d in range(1, n_aux):
                e_copy(d).start()

        return carry

    lax.fori_loop(0, pairs, step, 0)
    send_pair(pairs - 1)

    for d in range(1, n_aux):
        e_copy(d).wait_recv()
    for p in range(pairs_e):
        total = out_e[me, p]
        for d in range(1, n_aux):
            total = total + in_e[d - 1, p]
        keep = inside(rke[p], me * rows_e, (rows_e, full_e))
        oe[p] = jnp.where(
            keep, mine_e[p, :rows_e, :full_e] - total[:rows_e, :full_e] / den_e[p], F32(0.0)
        )

    for d in range(1, n_aux):
        pltpu.make_async_copy(in_a.at[d - 1], in_a.at[d - 1], a_recv.at[d - 1]).wait()
    for p in range(pairs):
        total = terms[p, me]
        for d in range(1, n_aux):
            total = total + in_a[d - 1, p].astype(F32)
        keep = inside(rka[p], me * rows, (rows, full))
        oa[p] = jnp.where(keep, mine[p].astype(F32) - total / den[p], F32(0.0))

    for d in range(1, n_pair):
        to_pair(d, my_pair).wait_send()
        to_pair_e(d, my_pair).wait_send()
    for d in range(1, n_aux):
        to_own(d, me).wait_send()
        e_copy(d).wait_send()
        pltpu.make_async_copy(in_a.at[d - 1], in_a.at[d - 1], a_send.at[d - 1]).wait()


def shards(n_pair, n_aux, *args):
    la, ra, aa = args[:3]
    ina = args[6]
    le, re, ae = args[9:12]
    pairs, rows, full = aa.shape
    pairs_e, rows_e, full_e = ae.shape
    pad_e = -(-rows_e // 8) * 8
    vmem = pl.BlockSpec(memory_space=pltpu.VMEM)
    smem = pl.BlockSpec(memory_space=pltpu.SMEM)
    hbm = pl.BlockSpec(memory_space=pl.ANY)
    dma = pltpu.SemaphoreType.DMA
    level = [hbm, hbm, vmem, smem, smem, vmem]
    return pl.pallas_call(
        functools.partial(kernel, n_pair, n_aux),
        out_shape=(
            jax.ShapeDtypeStruct(aa.shape, F32),
            jax.ShapeDtypeStruct(ae.shape, F32),
        ),
        in_specs=level + [hbm, smem, smem] + level + [vmem, smem, smem],
        out_specs=(vmem, vmem),
        scratch_shapes=[
            pltpu.VMEM(la.shape, BF),
            pltpu.VMEM(ra.shape, BF),
            pltpu.VMEM(le.shape, BF),
            pltpu.VMEM(re.shape, BF),
            pltpu.VMEM(ina.shape, BF),
            pltpu.VMEM((pairs, rows, full), BF),
            pltpu.VMEM((n_aux, pairs, rows, full), BF),
            pltpu.VMEM((n_pair * pairs, rows, full), BF),
            pltpu.VMEM((pairs_e, pad_e, LANES), F32),
            pltpu.VMEM((n_pair * pairs_e, pad_e, LANES), F32),
            pltpu.VMEM((pairs, n_aux, rows, full), F32),
            pltpu.VMEM((n_aux, pairs, rows, full), BF),
            pltpu.VMEM((n_aux - 1, pairs, rows, full), BF),
            pltpu.VMEM((pairs_e, full_e, full_e), F32),
            pltpu.VMEM((n_aux, pairs_e, pad_e, LANES), F32),
            pltpu.VMEM((n_aux - 1, pairs_e, pad_e, LANES), F32),
            pltpu.VMEM((pairs, rows, full), F32),
            pltpu.VMEM((pairs_e, rows_e, full_e), F32),
            dma((pairs, 2)),
            dma((2,)),
            dma,
            dma((n_aux - 1,)),
            dma((n_aux - 1,)),
            dma((n_pair - 1,)),
            dma((n_pair - 1,)),
            dma((n_pair - 1,)),
            dma((n_pair - 1,)),
            dma((n_aux - 1,)),
            dma((n_aux - 1,)),
            dma((n_aux - 1,)),
            dma((n_aux - 1,)),
        ],
        compiler_params=pltpu.CompilerParams(
            collective_id=0, has_side_effects=True, vmem_limit_bytes=60 * 1024 * 1024
        ),
        name="update",
    )(*args)


def solution(mesh):
    n_pair, n_aux = mesh.shape["pair"], mesh.shape["aux"]
    level = (
        P("pair", None, "aux"),
        P("pair", None, "aux"),
        P("pair", "aux", None),
        P("pair"),
        P("pair"),
        P("pair", None),
        P("pair", None, None, None),
        P("pair", None),
        P("pair", None),
    )
    return jax.shard_map(
        functools.partial(shards, n_pair, n_aux),
        mesh=mesh,
        in_specs=level + level,
        out_specs=(P("pair", "aux", None), P("pair", "aux", None)),
        check_vma=False,
    )
```

time: 193 us -> 45.9 us (0.24)
  blocking collectives: 82.3 us -> 0 us
  matrix products: 71.7 us -> 0 us
  Pallas kernels: 0 us -> 38.1 us
  between operations: 14.9 us -> 0.64 us
  waiting for transfers between devices: 12 us -> 0 us
  other arithmetic: 7.1 us -> 0 us
  local copies, waits for them, and re-layouts: 4.54 us -> 6.87 us
    dot_general x9 -> x0, matrix products: 71.7 us -> none  [the longest x2 18.5 us: aux_terms(): jnp.einsum('paq,pbq->pab', left_ints, right_ints, preferred_element_type=...]
    all_gather x3 -> x0, blocking collectives: 43.8 us -> none  [the longest x1 32.7 us: shards(): own_act = lax.all_gather(shard_act, 'aux', axis=1, tiled=True)]
    unnamed x1 -> x0, blocking collectives: 38.5 us -> none
    pallas_call x0 -> x1, Pallas kernels: none -> 38.1 us  [shards(): pl.pallas_call(functools.partial(kernel, n_pair, n_aux), out_shape=(jax.S...]
    reduce_scatter x1 -> x0, waiting for transfers between devices: 12 us -> none  [shards(): lax.psum_scatter(terms_act, 'aux', scatter_dimension=1, tiled=True)]
    select_n x6 -> x0, other arithmetic: 4.01 us -> none  [the longest x2 2.39 us: finish(): jnp.where(inside, amp_shard.astype(jnp.float32) - summed / denominator, j...]
    unnamed x22 -> x4, local copies, waits for them, and re-layouts: 2 us -> 5.54 us
    lt x4 -> x0, other arithmetic: 3.06 us -> none  [the longest x2 1.61 us: shard_mask(): col_index[None, None, :] < pair_ranks[:, None, None]]
  transfers between devices with their start and end apart: 1 -> 0, of which waited for: 1 -> 0; matrix products, arithmetic and copies ran while one was open for 5% -> 0% of each run, Pallas kernels for 0% -> 0%
where the time goes in v1:
time: 45.9 us; the launch traced here: 45.6 us
  Pallas kernels  38.1 us (83%)
  local copies, waits for them, and re-layouts  6.87 us (15%)
  between operations  0.64 us (1%)
    pallas_call x1, Pallas kernels, shards(): pl.pallas_call(functools.partial(kernel, n_pair, n_aux), out_shape=(jax.S...  38.1 us
    unnamed x4, local copies, waits for them, and re-layouts  5.54 us
    pallas_call x1, local copies, waits for them, and re-layouts, shards(): pl.pallas_call(functools.partial(kernel, n_pair, n_aux), out_shape=(jax.S...  1.32 us

profile of v1, /device:TPU:0, one launch (start us, length us, event | category | flops | bytes accessed | tf_op | source)
XLA Modules:
  0.0 45.6 jit_solution(7833586887742925555)
XLA Ops:
  0.6 1.4 %copy.20.fka = f32[10,4]{1,0:T(8,128)} copy(f32[10,4]{0,1:T(4,128)} %param.25) | data formatting | bytes 320 | tf_op args[7]
  2.0 1.4 %copy.21.nba = s32[10,4]{1,0:T(8,128)} copy(s32[10,4]{0,1:T(4,128)} %param.26) | data formatting | bytes 320 | tf_op args[8]
  3.4 1.3 %copy.22.ae = bf16[4,6,48]{2,1,0:T(8,128)(2,1)} copy(bf16[4,6,48]{2,0,1:T(4,128)(2,1)} %param.29) | data formatting | bytes 4608 | tf_op args[11]
  4.6 38.1 %update.1 = (f32[10,16,128]{2,1,0:T(8,128)}, f32[4,6,48]{2,1,0:T(8,128)}) custom-call(bf16[10,128,7680]{2,1,0:T(8,128)(2,1)} %la.1, bf16[10,128,7680]{2,1,0:T(8,128)(2,1)} %ra.1, bf16[10,16,128]{2,1,0:T(8,128)(2,1)} %aa.1, s32[10]{0:T(128)} %rka.1, f32[10]{0:T(128)} %gpa.1, f32[10,128]{1,0:T(8,128)} %ena.1, bf16[10,4,128,128]{3,2,1,0:T(8,128)(2,1)} %ina.1, ...), custom_call_target="tpu_custom_call" | custom-call | tf_op jit(solution)/shard_map/update/pallas_call | solution.py:284
  42.8 1.3 %copy.23 = f32[4,6,48]{2,0,1:T(4,128)} copy(f32[4,6,48]{2,1,0:T(8,128)} %get-tuple-element.3) | data formatting | bytes 9216 | tf_op jit(solution)/shard_map/update/pallas_call | solution.py:284
  44.1 1.5 %copy.25 = f32[10,16,128]{2,1,0:T(8,128)} copy(f32[10,16,128]{2,1,0:T(8,128)} %get-tuple-element.6) | data formatting | bytes 163840
